TPU v7x, 32 devices: a whole 2x2x4 slice. The times are simulated.
32 devices in a mesh: fsdp: 4 (over y, x), seq: 8 (over z, core).
Axes of the slice: x: 2, y: 2, z: 4, core: 2. Of those that a mesh axis runs over, the one named last changes fastest.
Arguments:
- q_next: bfloat16 [4096, 4096], P(('fsdp', 'seq')), may hold values from -9 to 9
- k_next: bfloat16 [4096, 1024], P(('fsdp', 'seq')), may hold values from -4 to 4
- v_next: bfloat16 [4096, 1024], P(('fsdp', 'seq')), may hold values from -6 to 6
- seg_next: int32 [4, 1024], P('fsdp'), may hold values from 0 to 3, never falling along the last dimension, each value on 1 to 512 neighbouring positions
- q_prev: bfloat16 [4096, 4096], P(('fsdp', 'seq')), may hold values from -9 to 9
- k_prev: bfloat16 [4096, 1024], P(('fsdp', 'seq')), may hold values from -4 to 4
- v_prev: bfloat16 [4096, 1024], P(('fsdp', 'seq')), may hold values from -6 to 6
- seg_prev: int32 [4, 1024], P('fsdp'), may hold values from 0 to 3, never falling along the last dimension, each value on 1 to 512 neighbouring positions
- upstream: bfloat16 [4096, 4096], P(('fsdp', 'seq')), may hold values from -6 to 6
- flags: int32 [4, 1024], P('fsdp', 'seq'), may hold values from 0 to 1
Outputs:
- attn_next: bfloat16 [4096, 4096], P(('fsdp', 'seq'))
- grad_q: bfloat16 [4096, 4096], P(('fsdp', 'seq'))
- grad_k: bfloat16 [4096, 1024], P(('fsdp', 'seq'))
- grad_v: bfloat16 [4096, 1024], P(('fsdp', 'seq'))
Inputs may be any that keep to these rules, and one draw needn't show every extreme that they name: `seg_next`: within each sequence the ids never fall and each id covers at most 512 consecutive positions; some id covers exactly 512. `seg_prev`: within each sequence the ids never fall and each id covers at most 512 consecutive positions; some id covers exactly 512.
All inputs are finite; a program needn't handle non-finite values.
Results may differ from a plain program's by a relative error of at most 0.0067.
Values may be sent and summed in bfloat16 or wider, within the bound.
No kernel may reach another device: no remote copies, remote signals or barrier semaphores. Data moves between devices by JAX's collectives and lax.ppermute only.
A program may use at most 128 MiB of HBM per device.

v0:
```python
import jax
import jax.numpy as jnp
from jax import lax
from jax.sharding import PartitionSpec as P

HEAD_DIM = 128


def passed_along(block, axis, distance):
    devices = range(lax.axis_size(axis))
    route = [(i - distance, i) for i in devices if i - distance in devices]
    return lax.ppermute(block, axis, route)


def masked_probs(q_block, k_window, q_pos, k_pos, q_seg, k_seg, scale_factor):
    scores = (
        jnp.einsum("qhd,khd->hqk", q_block, k_window, preferred_element_type=jnp.float32)
        * scale_factor
    )
    keep_mask = (k_seg[None, :] == q_seg[:, None]) & (k_pos[None, :] <= q_pos[:, None])
    scores = jnp.where(keep_mask[None], scores, -1e30)
    row_max = jnp.max(scores, axis=-1, keepdims=True)
    expo_vals = jnp.exp(scores - row_max)
    return expo_vals / jnp.sum(expo_vals, axis=-1, keepdims=True)


def block_window(seq_ids, block_start, block_len, reach):
    padded = jnp.concatenate([jnp.full((reach,), -1, jnp.int32), seq_ids])
    q_seg = lax.dynamic_slice_in_dim(seq_ids, block_start, block_len)
    k_seg = lax.dynamic_slice_in_dim(padded, block_start, reach + block_len)
    q_pos = block_start + jnp.arange(block_len, dtype=jnp.int32)
    k_pos = block_start - reach + jnp.arange(reach + block_len, dtype=jnp.int32)
    return (q_pos, k_pos, q_seg, k_seg)


def pad_front(array, reach):
    return jnp.concatenate([jnp.zeros((reach,) + array.shape[1:], array.dtype), array], axis=0)


def forward_heads(q_heads, k_heads, v_heads, seq_ids, reach, block_len, scale_factor):
    seq_len = q_heads.shape[0]
    k_padded = pad_front(k_heads, reach)
    v_padded = pad_front(v_heads, reach)

    def block_step(block_idx, output):
        block_start = (block_idx * block_len).astype(jnp.int32)
        q_pos, k_pos, q_seg, k_seg = block_window(seq_ids, block_start, block_len, reach)
        q_block = lax.dynamic_slice_in_dim(q_heads, block_start, block_len, 0)
        k_window = lax.dynamic_slice_in_dim(k_padded, block_start, reach + block_len, 0)
        v_window = lax.dynamic_slice_in_dim(v_padded, block_start, reach + block_len, 0)
        soft_probs = masked_probs(q_block, k_window, q_pos, k_pos, q_seg, k_seg, scale_factor)
        result = jnp.einsum(
            "hqk,khd->qhd",
            soft_probs.astype(jnp.bfloat16),
            v_window,
            preferred_element_type=jnp.float32,
        )
        return lax.dynamic_update_slice_in_dim(output, result.astype(jnp.bfloat16), block_start, 0)

    return lax.fori_loop(
        0, seq_len // block_len, block_step, jnp.zeros(q_heads.shape, jnp.bfloat16)
    )


def window_meta(seq_ids, rows_here, hop_total):
    width_all = (hop_total + 1) * rows_here
    first_row = lax.axis_index("seq") * rows_here
    padded = jnp.concatenate([jnp.full((hop_total * rows_here,), -1, jnp.int32), seq_ids])
    k_seg = lax.dynamic_slice_in_dim(padded, first_row, width_all)
    q_seg = lax.dynamic_slice_in_dim(seq_ids, first_row, rows_here)
    q_pos = first_row + jnp.arange(rows_here, dtype=jnp.int32)
    k_pos = first_row - hop_total * rows_here + jnp.arange(width_all, dtype=jnp.int32)
    keep_mask = (k_seg[None, :] == q_seg[:, None]) & (k_pos[None, :] <= q_pos[:, None])
    return keep_mask


def grouped_probs(grouped, k_window, keep_mask, scale_factor):
    scores = (
        jnp.einsum("qjgd,kjd->jgqk", grouped, k_window, preferred_element_type=jnp.float32)
        * scale_factor
    )
    scores = jnp.where(keep_mask[None, None], scores, -1e30)
    row_max = jnp.max(scores, axis=-1, keepdims=True)
    expo_vals = jnp.exp(scores - row_max)
    return expo_vals / jnp.sum(expo_vals, axis=-1, keepdims=True)


def backward_local(q_local, k_local, v_local, d_local, seq_ids, reach, scale_factor):
    rows_here = q_local.shape[0]
    head_dim = HEAD_DIM
    heads_all = q_local.shape[1] // head_dim
    kv_heads = k_local.shape[1] // head_dim
    group_size = heads_all // kv_heads
    hop_total = (reach + rows_here - 1) // rows_here
    key_list = [k_local]
    value_list = [v_local]
    for hop_count in range(1, hop_total + 1):
        far_keys, far_values = passed_along((k_local, v_local), "seq", hop_count)
        key_list.insert(0, far_keys)
        value_list.insert(0, far_values)
    width_all = (hop_total + 1) * rows_here
    k_window = jnp.concatenate(key_list, axis=0).reshape(width_all, kv_heads, head_dim)
    v_window = jnp.concatenate(value_list, axis=0).reshape(width_all, kv_heads, head_dim)
    keep_mask = window_meta(seq_ids, rows_here, hop_total)
    grouped_q = q_local.reshape(rows_here, kv_heads, group_size, head_dim)
    grouped_d = d_local.reshape(rows_here, kv_heads, group_size, head_dim)
    soft_probs = grouped_probs(grouped_q, k_window, keep_mask, scale_factor)
    d_probs = jnp.einsum("qjgd,kjd->jgqk", grouped_d, v_window, preferred_element_type=jnp.float32)
    row_delta = jnp.sum(soft_probs * d_probs, axis=-1, keepdims=True)
    d_scores = (soft_probs * (d_probs - row_delta) * scale_factor).astype(jnp.bfloat16)
    q_grad = jnp.einsum("jgqk,kjd->qjgd", d_scores, k_window, preferred_element_type=jnp.float32)
    q_grad = q_grad.astype(jnp.bfloat16).reshape(rows_here, heads_all * head_dim)
    k_term = jnp.einsum(
        "jgqk,qjgd->kjd", d_scores, grouped_q, preferred_element_type=jnp.float32
    ).reshape(width_all, kv_heads * head_dim)
    v_term = jnp.einsum(
        "jgqk,qjgd->kjd",
        soft_probs.astype(jnp.bfloat16),
        grouped_d,
        preferred_element_type=jnp.float32,
    ).reshape(width_all, kv_heads * head_dim)
    k_total = k_term[hop_total * rows_here :]
    v_total = v_term[hop_total * rows_here :]
    for hop_count in range(1, hop_total + 1):
        start_row = (hop_total - hop_count) * rows_here
        back_keys, back_values = passed_along(
            (k_term[start_row : start_row + rows_here], v_term[start_row : start_row + rows_here]),
            "seq",
            -hop_count,
        )
        k_total = k_total + back_keys
        v_total = v_total + back_values
    return (q_grad, k_total.astype(jnp.bfloat16), v_total.astype(jnp.bfloat16))


def body(q_next, k_next, v_next, seg_next, q_prev, k_prev, v_prev, seg_prev, upstream, flags):
    rows_here = q_next.shape[0]
    head_dim = HEAD_DIM
    heads_all = q_next.shape[1] // head_dim
    kv_heads = k_next.shape[1] // head_dim
    group_size = heads_all // kv_heads
    seq_size = lax.axis_size("seq")
    seq_len = rows_here * seq_size
    token_total = rows_here * lax.axis_size("fsdp") * seq_size
    reach = min(512, 4 * rows_here, seq_len // 2)
    block_len = min(512, seq_len)
    scale_factor = head_dim ** (-0.5)
    heads_here = heads_all // seq_size
    next_ids = seg_next[0]
    prev_ids = seg_prev[0]
    flag_total = lax.psum(jnp.sum(flags.astype(jnp.float32)), ("fsdp", "seq"))
    weight = flags.reshape(rows_here, 1).astype(jnp.float32) * (
        token_total / jnp.maximum(flag_total, 1.0)
    )
    cotangent = (upstream.astype(jnp.float32) * weight).astype(jnp.bfloat16)

    def shared_heads(array):
        split_heads = array.reshape(rows_here, kv_heads, head_dim)
        return jnp.repeat(split_heads, group_size, axis=1).reshape(rows_here, heads_all * head_dim)

    def as_heads(array):
        return array.reshape(seq_len, heads_here, head_dim)

    next_in = (
        lax.all_to_all(q_next, "seq", split_axis=1, concat_axis=0, tiled=True),
        lax.all_to_all(shared_heads(k_next), "seq", split_axis=1, concat_axis=0, tiled=True),
        lax.all_to_all(shared_heads(v_next), "seq", split_axis=1, concat_axis=0, tiled=True),
    )
    out_heads = forward_heads(
        as_heads(next_in[0]),
        as_heads(next_in[1]),
        as_heads(next_in[2]),
        next_ids,
        reach,
        block_len,
        scale_factor,
    )
    attn_next = lax.all_to_all(
        out_heads.reshape(seq_len, heads_here * head_dim),
        "seq",
        split_axis=0,
        concat_axis=1,
        tiled=True,
    )
    grad_q, grad_k, grad_v = backward_local(
        q_prev, k_prev, v_prev, cotangent, prev_ids, reach, scale_factor
    )
    return (attn_next, grad_q, grad_k, grad_v)


def solution(mesh):
    return jax.shard_map(
        body,
        mesh=mesh,
        in_specs=(
            P(("fsdp", "seq"), None),
            P(("fsdp", "seq"), None),
            P(("fsdp", "seq"), None),
            P("fsdp", None),
            P(("fsdp", "seq"), None),
            P(("fsdp", "seq"), None),
            P(("fsdp", "seq"), None),
            P("fsdp", None),
            P(("fsdp", "seq"), None),
            P("fsdp", "seq"),
        ),
        out_specs=(
            P(("fsdp", "seq"), None),
            P(("fsdp", "seq"), None),
            P(("fsdp", "seq"), None),
            P(("fsdp", "seq"), None),
        ),
        check_vma=False,
    )
```

profile of v0, /device:TPU:0, one launch (start us, length us, event | category | flops | bytes accessed | tf_op | source)
XLA Modules:
  0.0 330.4 jit_solution(18408808824649141956)
XLA Ops:
  3.1 6.4 %all-to-all-start = ((bf16[128,8,512]{0,2,1:T(8,128)(2,1)}), bf16[128,8,512]{0,2,1:T(8,128)(2,1)S(1)}, u32[]{:S(2)}, u32[]{:S(2)}) async-start(bf16[128,8,512]{0,2,1:T(8,128)(2,1)} %bitcast.2), calls=%async_computation | async-start | bytes 2097152 | tf_op jit(solution)/shard_map/all_to_all | solution.py:167
  9.4 1.8 copy.126
  11.2 3.1 collective-permute-start.7
  14.3 3.6 %collective-permute-start.6 = (bf16[128,1024]{0,1:T(8,128)(2,1)}, bf16[128,1024]{0,1:T(8,128)(2,1)}, u32[]{:S(2)}, u32[]{:S(2)}) collective-permute-start(bf16[128,1024]{0,1:T(8,128)(2,1)} %copy.126), channel_id=1, source_target_pairs={{0,2},{1,3},{2,4},{3,5},{4,6},{5,7},{8,10},{9,11},{10,12},{11,13},... | collective-permute-start | bytes 786440 | tf_op jit(solution)/shard_map/ppermute | solution.py:12
  19.0 3.4 %collective-permute-start.2 = (bf16[128,1024]{0,1:T(8,128)(2,1)S(1)}, bf16[128,1024]{0,1:T(8,128)(2,1)}, u32[]{:S(2)}, u32[]{:S(2)}) collective-permute-start(bf16[128,1024]{0,1:T(8,128)(2,1)S(1)} %copy.119), channel_id=1, source_target_pairs={{0,2},{1,3},{2,4},{3,5},{4,6},{5,7},{8,10},{9,11},{10,12},{11,13},... | collective-permute-start | bytes 786440 | tf_op jit(solution)/shard_map/ppermute | solution.py:12
  22.4 2.7 collective-permute-start.1
  26.4 2.0 collective-permute-start
  28.4 58.8 %psum.7 = f32[]{:T(128)} all-reduce(f32[]{:T(128)} %convert_reduce_fusion), channel_id=1, replica_groups=mesh['fsdp'=4,'seq'=8] {'fsdp','seq'}, use_global_device_ids=true, to_apply=%region_7.8 | all-reduce | flops 1 | bytes 8 | tf_op jit(solution)/shard_map/psum | solution.py:151
  91.7 4.3 %all-to-all-start.2 = ((bf16[128,8,512]{0,2,1:T(8,128)(2,1)}), bf16[128,8,512]{0,2,1:T(8,128)(2,1)}, u32[]{:S(2)}, u32[]{:S(2)}) async-start(bf16[128,8,512]{0,2,1:T(8,128)(2,1)} %bitcast.8), calls=%async_computation.2 | async-start | bytes 2097152 | tf_op jit(solution)/shard_map/all_to_all | solution.py:166
  97.8 2.6 copy.111
  100.4 2.3 copy.167
  102.7 2.3 collective-permute-start.3
  106.0 4.6 %collective-permute-start.5 = (bf16[128,1024]{0,1:T(8,128)(2,1)}, bf16[128,1024]{0,1:T(8,128)(2,1)S(1)}, u32[]{:S(2)}, u32[]{:S(2)}) collective-permute-start(bf16[128,1024]{0,1:T(8,128)(2,1)} %copy.126), channel_id=1, source_target_pairs={{0,3},{1,4},{2,5},{3,6},{4,7},{8,11},{9,12},{10,13},{11,14},{12,15... | collective-permute-start | bytes 786440 | tf_op jit(solution)/shard_map/ppermute | solution.py:12
  111.7 2.2 collective-permute-start.4
  115.1 10.4 %collective-permute-done.4 = bf16[128,1024]{0,1:T(8,128)(2,1)S(1)} collective-permute-done((bf16[128,1024]{0,1:T(8,128)(2,1)}, bf16[128,1024]{0,1:T(8,128)(2,1)S(1)}, u32[]{:S(2)}, u32[]{:S(2)}) %collective-permute-start.4) | collective-permute-done | bytes 262176 | tf_op jit(solution)/shard_map/ppermute | solution.py:12
  126.6 21.4 %all-to-all-start.1 = ((bf16[128,8,512]{0,2,1:T(8,128)(2,1)}), bf16[128,8,512]{0,2,1:T(8,128)(2,1)}, u32[]{:S(2)}, u32[]{:S(2)}) async-start(bf16[128,8,512]{0,2,1:T(8,128)(2,1)} %bitcast.5), calls=%async_computation.1 | async-start | bytes 2097152 | tf_op jit(solution)/shard_map/all_to_all | solution.py:165
  150.1 5.5 %fusion.48 = f32[8,640,128,4]{2,1,3,0:T(8,128)} fusion(bf16[640,8,128,1]{0,2,3,1:T(8,128)(2,1)S(1)} %bitcast.138, bf16[128,8,4,128]{0,3,2,1:T(8,128)(2,1)S(1)} %bitcast.122), kind=kOutput, calls=%fused_computation.77 | convolution fusion | flops 671088640 | bytes 12845056 | tf_op jit(solution)/shard_map/qjgd,kjd->jgqk/dot_general | solution.py:108
  155.7 9.1 %fusion.47 = (f32[8,4,128]{2,1,0:T(4,128)S(1)}, f32[8,4,128,640]{2,3,1,0:T(8,128)}) fusion(pred[128,640]{0,1:T(8,128)(4,1)S(1)} %compare_and_fusion.1, bf16[640,8,128,1]{0,2,3,1:T(8,128)(2,1)} %bitcast.145, bf16[128,8,4,128]{0,3,2,1:T(8,128)(2,1)} %bitcast.141), kind=kOutput, calls=%fused_computation.76 | convolution fusion | flops 681575040 | bytes 12943360 | tf_op jit(solution)/shard_map/sub | solution.py:84
  164.7 16.4 %fusion.34 = f32[640,8,128]{0,2,1:T(8,128)} fusion(bf16[128,8,4,128]{0,3,2,1:T(8,128)(2,1)S(1)} %bitcast.142, f32[8,640,128,4]{2,1,3,0:T(8,128)} %fusion.48, f32[8,4,128,640]{2,3,1,0:T(8,128)} %get-tuple-element.220, f32[8,4,128]{2,1,0:T(4,128)S(1)} %get-tuple-element.219), kind=kOutput, calls=%fused_computation.45 | convolution fusion | flops 689443456 | bytes 24657920 | tf_op jit(solution)/shard_map/jgqk,qjgd->kjd/dot_general | solution.py:113
  181.1 2.7 fusion.46
  189.5 1.5 collective-permute-start.11
  192.1 2.9 copy.114
  195.0 1.5 reshape.227
  196.5 1.3 concatenate.20
  198.0 2.9 copy.112
  200.9 1.5 reshape.225
  203.5 27.9 %while.15 = (s32[]{:T(128)}, bf16[1024,4,128]{0,2,1:T(8,128)(2,1)}, bf16[1536,4,128]{0,2,1:T(8,128)(2,1)}, s32[1024]{0:T(1024)S(1)}, bf16[1024,4,128]{0,2,1:T(8,...) while((s32[]{:T(128)}, bf16[1024,4,128]{0,2,1:T(8,128)(2,1)}, ...), condition=%wide.region_3.0_spmd, body=%wide.region_0.3_spmd.sunk | while | flops 1092356608 | bytes 52476220 | solution.py:60
  204.2 1.3 fusion.67
  205.5 6.0 %fusion.68 = (f32[4,512]{1,0:T(4,128)S(1)}, f32[4,512,1024]{2,1,0:T(8,128)}) fusion(f32[4,512,1024]{2,1,0:T(8,128)S(1)} %fusion.67, pred[512,1024]{1,0:T(8,128)(4,1)S(1)} %compare_and_fusion.3), kind=kOutput, calls=%fused_computation.73.clone.1 | output fusion | flops 12583935 | bytes 17309696 | tf_op jit(solution)/shard_map/while/body/eval_jaxpr/sub | solution.py:23
  211.5 5.0 %fusion.69 = bf16[1024,4,128]{0,2,1:T(8,128)(2,1)S(1)} fusion(bf16[1024,4,128]{0,2,1:T(8,128)(2,1)S(1)} %copy-done.1, s32[]{:T(128)S(6)} %select_n.72, f32[4,512,1024]{2,1,0:T(8,128)} %get-tuple-element.266, f32[4,512]{1,0:T(4,128)S(1)} %get-tuple-element.267, bf16[1536,4,128]{0,2,1:T(8,128)(2,1)S(1)} %copy-done.4, s32[]{:T(128)S(6)} %select_n.73), kind=kOutput, calls=%fused_computation.12.clone.1 | convolution fusion | flops 541327360 | bytes 9969672 | tf_op jit(solution)/shard_map/while/body/eval_jaxpr/hqk,khd->qhd/dot_general | solution.py:52
  218.1 1.3 fusion.67
  219.4 6.0 %fusion.68 = (f32[4,512]{1,0:T(4,128)S(1)}, f32[4,512,1024]{2,1,0:T(8,128)}) fusion(f32[4,512,1024]{2,1,0:T(8,128)S(1)} %fusion.67, pred[512,1024]{1,0:T(8,128)(4,1)S(1)} %compare_and_fusion.3), kind=kOutput, calls=%fused_computation.73.clone.1 | output fusion | flops 12583935 | bytes 17309696 | tf_op jit(solution)/shard_map/while/body/eval_jaxpr/sub | solution.py:23
  225.4 5.0 %fusion.69 = bf16[1024,4,128]{0,2,1:T(8,128)(2,1)S(1)} fusion(bf16[1024,4,128]{0,2,1:T(8,128)(2,1)S(1)} %copy-done.1, s32[]{:T(128)S(6)} %select_n.72, f32[4,512,1024]{2,1,0:T(8,128)} %get-tuple-element.266, f32[4,512]{1,0:T(4,128)S(1)} %get-tuple-element.267, bf16[1536,4,128]{0,2,1:T(8,128)(2,1)S(1)} %copy-done.4, s32[]{:T(128)S(6)} %select_n.73), kind=kOutput, calls=%fused_computation.12.clone.1 | convolution fusion | flops 541327360 | bytes 9969672 | tf_op jit(solution)/shard_map/while/body/eval_jaxpr/hqk,khd->qhd/dot_general | solution.py:52
  231.4 1.5 copy.169
  232.9 1.5 copy.160
  234.4 8.8 %all-to-all-start.3 = ((bf16[8,128,512]{2,1,0:T(8,128)(2,1)}), bf16[8,128,512]{2,1,0:T(8,128)(2,1)S(1)}, u32[]{:S(2)}, u32[]{:S(2)}) async-start(bf16[8,128,512]{2,1,0:T(8,128)(2,1)} %copy.160), calls=%async_computation.3 | async-start | bytes 2097152 | tf_op jit(solution)/shard_map/all_to_all | solution.py:178
  243.2 7.6 %fusion.31 = f32[640,8,128]{0,2,1:T(8,128)} fusion(bf16[128,8,4,128]{0,3,2,1:T(8,128)(2,1)} %bitcast.123, f32[8,4,128,640]{2,3,1,0:T(8,128)} %get-tuple-element.220, f32[8,4,128]{2,1,0:T(4,128)S(1)} %get-tuple-element.219), kind=kOutput, calls=%fused_computation.44 | convolution fusion | flops 676331520 | bytes 14172160 | tf_op jit(solution)/shard_map/jgqk,qjgd->kjd/dot_general | solution.py:116
  253.1 2.9 fusion.45
  256.0 2.0 copy.143
  258.0 2.0 copy.147
  266.0 1.5 collective-permute-start.12
  267.5 15.3 %fusion.35 = bf16[8,128,4,128]{3,1,2,0:T(8,128)(2,1)S(1)} fusion(bf16[640,8,128,1]{0,2,3,1:T(8,128)(2,1)} %bitcast.146, f32[8,640,128,4]{2,1,3,0:T(8,128)} %fusion.48, f32[8,4,128,640]{2,3,1,0:T(8,128)} %get-tuple-element.220, f32[8,4,128]{2,1,0:T(4,128)S(1)} %get-tuple-element.219), kind=kOutput, calls=%fused_computation.46 | convolution fusion | flops 689967744 | bytes 23347200 | tf_op jit(solution)/shard_map/jgqk,kjd->qjgd/dot_general | solution.py:111
  282.8 1.3 copy.149
  284.5 2.4 add_convert_fusion.1
  286.9 5.5 %collective-permute-done.14 = f32[128,1024]{1,0:T(8,128)} collective-permute-done((f32[128,1024]{1,0:T(8,128)}, f32[128,1024]{1,0:T(8,128)}, u32[]{:S(2)}, u32[]{:S(2)}) %collective-permute-start.14) | collective-permute-done | bytes 524320 | tf_op jit(solution)/shard_map/ppermute | solution.py:12
  292.4 33.7 %collective-permute-done.15 = f32[128,1024]{1,0:T(8,128)} collective-permute-done((f32[128,1024]{1,0:T(8,128)}, f32[128,1024]{1,0:T(8,128)}, u32[]{:S(2)}, u32[]{:S(2)}) %collective-permute-start.15) | collective-permute-done | bytes 524320 | tf_op jit(solution)/shard_map/ppermute | solution.py:12
  326.0 2.4 add_convert_fusion
  329.1 1.3 copy.148
  (91 shorter events, 37.2 us)
Async XLA Ops:
  0.6 95.3 %copy-start.5 = (bf16[128,4096]{1,0:T(8,128)(2,1)S(1)}, bf16[128,4096]{1,0:T(8,128)(2,1)}, u32[]{:S(2)}) copy-start(bf16[128,4096]{1,0:T(8,128)(2,1)} %param.20) | copy-start | bytes 3145732
  3.1 87.4 %all-to-all-start = ((bf16[128,8,512]{0,2,1:T(8,128)(2,1)}), bf16[128,8,512]{0,2,1:T(8,128)(2,1)S(1)}, u32[]{:S(2)}, u32[]{:S(2)}) async-start(bf16[128,8,512]{0,2,1:T(8,128)(2,1)} %bitcast.2), calls=%async_computation | async-start | bytes 2097152 | tf_op jit(solution)/shard_map/all_to_all | solution.py:167
  11.2 136.9 %collective-permute-start.7 = (bf16[128,1024]{0,1:T(8,128)(2,1)}, bf16[128,1024]{0,1:T(8,128)(2,1)}, u32[]{:S(2)}, u32[]{:S(2)}) collective-permute-start(bf16[128,1024]{0,1:T(8,128)(2,1)} %copy.126), channel_id=1, source_target_pairs={{0,1},{1,2},{2,3},{3,4},{4,5},{5,6},{6,7},{8,9},{9,10},{10,11},{11... | collective-permute-start | bytes 786440 | tf_op jit(solution)/shard_map/ppermute | solution.py:12
  14.3 111.3 %collective-permute-start.6 = (bf16[128,1024]{0,1:T(8,128)(2,1)}, bf16[128,1024]{0,1:T(8,128)(2,1)}, u32[]{:S(2)}, u32[]{:S(2)}) collective-permute-start(bf16[128,1024]{0,1:T(8,128)(2,1)} %copy.126), channel_id=1, source_target_pairs={{0,2},{1,3},{2,4},{3,5},{4,6},{5,7},{8,10},{9,11},{10,12},{11,13},... | collective-permute-start | bytes 786440 | tf_op jit(solution)/shard_map/ppermute | solution.py:12
  19.0 92.6 %collective-permute-start.2 = (bf16[128,1024]{0,1:T(8,128)(2,1)S(1)}, bf16[128,1024]{0,1:T(8,128)(2,1)}, u32[]{:S(2)}, u32[]{:S(2)}) collective-permute-start(bf16[128,1024]{0,1:T(8,128)(2,1)S(1)} %copy.119), channel_id=1, source_target_pairs={{0,2},{1,3},{2,4},{3,5},{4,6},{5,7},{8,10},{9,11},{10,12},{11,13},... | collective-permute-start | bytes 786440 | tf_op jit(solution)/shard_map/ppermute | solution.py:12
  22.4 83.6 %collective-permute-start.1 = (bf16[128,1024]{0,1:T(8,128)(2,1)S(1)}, bf16[128,1024]{0,1:T(8,128)(2,1)}, u32[]{:S(2)}, u32[]{:S(2)}) collective-permute-start(bf16[128,1024]{0,1:T(8,128)(2,1)S(1)} %copy.119), channel_id=1, source_target_pairs={{0,3},{1,4},{2,5},{3,6},{4,7},{8,11},{9,12},{10,13},{11,14},{12,15... | collective-permute-start | bytes 786440 | tf_op jit(solution)/shard_map/ppermute | solution.py:12
  26.4 76.3 %collective-permute-start = (bf16[128,1024]{0,1:T(8,128)(2,1)S(1)}, bf16[128,1024]{0,1:T(8,128)(2,1)}, u32[]{:S(2)}, u32[]{:S(2)}) collective-permute-start(bf16[128,1024]{0,1:T(8,128)(2,1)S(1)} %copy.119), channel_id=1, source_target_pairs={{0,4},{1,5},{2,6},{3,7},{8,12},{9,13},{10,14},{11,15},{16,20},{17,... | collective-permute-start | bytes 786440 | tf_op jit(solution)/shard_map/ppermute | solution.py:12
  91.7 35.0 %all-to-all-start.2 = ((bf16[128,8,512]{0,2,1:T(8,128)(2,1)}), bf16[128,8,512]{0,2,1:T(8,128)(2,1)}, u32[]{:S(2)}, u32[]{:S(2)}) async-start(bf16[128,8,512]{0,2,1:T(8,128)(2,1)} %bitcast.8), calls=%async_computation.2 | async-start | bytes 2097152 | tf_op jit(solution)/shard_map/all_to_all | solution.py:166
  97.8 57.9 %copy-start = (bf16[128,4096]{0,1:T(8,128)(2,1)}, bf16[128,4096]{0,1:T(8,128)(2,1)S(1)}, u32[]{:S(2)}) copy-start(bf16[128,4096]{0,1:T(8,128)(2,1)S(1)} %copy.168) | copy-start | bytes 3145732
  102.7 12.2 %collective-permute-start.3 = (bf16[128,1024]{0,1:T(8,128)(2,1)S(1)}, bf16[128,1024]{0,1:T(8,128)(2,1)S(1)}, u32[]{:S(2)}, u32[]{:S(2)}) collective-permute-start(bf16[128,1024]{0,1:T(8,128)(2,1)S(1)} %copy.119), channel_id=1, source_target_pairs={{0,1},{1,2},{2,3},{3,4},{4,5},{5,6},{6,7},{8,9},{9,10},{10,11},{11... | collective-permute-start | bytes 786440 | tf_op jit(solution)/shard_map/ppermute | solution.py:12
  106.0 19.5 %collective-permute-start.5 = (bf16[128,1024]{0,1:T(8,128)(2,1)}, bf16[128,1024]{0,1:T(8,128)(2,1)S(1)}, u32[]{:S(2)}, u32[]{:S(2)}) collective-permute-start(bf16[128,1024]{0,1:T(8,128)(2,1)} %copy.126), channel_id=1, source_target_pairs={{0,3},{1,4},{2,5},{3,6},{4,7},{8,11},{9,12},{10,13},{11,14},{12,15... | collective-permute-start | bytes 786440 | tf_op jit(solution)/shard_map/ppermute | solution.py:12
  111.7 13.8 %collective-permute-start.4 = (bf16[128,1024]{0,1:T(8,128)(2,1)}, bf16[128,1024]{0,1:T(8,128)(2,1)S(1)}, u32[]{:S(2)}, u32[]{:S(2)}) collective-permute-start(bf16[128,1024]{0,1:T(8,128)(2,1)} %copy.126), channel_id=1, source_target_pairs={{0,4},{1,5},{2,6},{3,7},{8,12},{9,13},{10,14},{11,15},{16,20},{17,... | collective-permute-start | bytes 786440 | tf_op jit(solution)/shard_map/ppermute | solution.py:12
  115.0 10.6 %copy-start.8 = (bf16[640,1024]{0,1:T(8,128)(2,1)}, bf16[640,1024]{0,1:T(8,128)(2,1)S(1)}, u32[]{:S(2)}) copy-start(bf16[640,1024]{0,1:T(8,128)(2,1)S(1)} %constant_dynamic-update-slice_fusion) | copy-start | bytes 3932164
  126.6 71.4 %all-to-all-start.1 = ((bf16[128,8,512]{0,2,1:T(8,128)(2,1)}), bf16[128,8,512]{0,2,1:T(8,128)(2,1)}, u32[]{:S(2)}, u32[]{:S(2)}) async-start(bf16[128,8,512]{0,2,1:T(8,128)(2,1)} %bitcast.5), calls=%async_computation.1 | async-start | bytes 2097152 | tf_op jit(solution)/shard_map/all_to_all | solution.py:165
  155.7 9.1 %copy-start.6 = (bf16[128,4096]{0,1:T(8,128)(2,1)S(1)}, bf16[128,4096]{0,1:T(8,128)(2,1)}, u32[]{:S(2)}) copy-start(bf16[128,4096]{0,1:T(8,128)(2,1)} %copy.167) | copy-start | bytes 3145732
  186.9 76.5 %collective-permute-start.9 = (f32[128,1024]{1,0:T(8,128)}, f32[128,1024]{1,0:T(8,128)}, u32[]{:S(2)}, u32[]{:S(2)}) collective-permute-start(f32[128,1024]{1,0:T(8,128)} %copy.138), channel_id=1, source_target_pairs={{2,0},{3,1},{4,2},{5,3},{6,4},{7,5},{10,8},{11,9},{12,10},{13,11},... | collective-permute-start | bytes 1572872 | tf_op jit(solution)/shard_map/ppermute | solution.py:12
  188.2 76.5 %collective-permute-start.10 = (f32[128,1024]{1,0:T(8,128)}, f32[128,1024]{1,0:T(8,128)}, u32[]{:S(2)}, u32[]{:S(2)}) collective-permute-start(f32[128,1024]{1,0:T(8,128)} %copy.139), channel_id=1, source_target_pairs={{3,0},{4,1},{5,2},{6,3},{7,4},{11,8},{12,9},{13,10},{14,11},{15,12... | collective-permute-start | bytes 1572872 | tf_op jit(solution)/shard_map/ppermute | solution.py:12
  189.5 76.5 %collective-permute-start.11 = (f32[128,1024]{1,0:T(8,128)}, f32[128,1024]{1,0:T(8,128)}, u32[]{:S(2)}, u32[]{:S(2)}) collective-permute-start(f32[128,1024]{1,0:T(8,128)} %copy.140), channel_id=1, source_target_pairs={{4,0},{5,1},{6,2},{7,3},{12,8},{13,9},{14,10},{15,11},{20,16},{21,... | collective-permute-start | bytes 1572872 | tf_op jit(solution)/shard_map/ppermute | solution.py:12
  191.6 11.9 %copy-start.7 = (s32[1,1024]{1,0:T(1,128)S(1)}, s32[1,1024]{1,0:T(1,128)}, u32[]{:S(2)}) copy-start(s32[1,1024]{1,0:T(1,128)} %param.15) | copy-start | bytes 12292
  205.5 6.0 %copy-start.1 = (bf16[1024,4,128]{0,2,1:T(8,128)(2,1)S(1)}, bf16[1024,4,128]{0,2,1:T(8,128)(2,1)}, u32[]{:S(2)}) copy-start(bf16[1024,4,128]{0,2,1:T(8,128)(2,1)} %get-tuple-element.281) | copy-start | bytes 3145732 | tf_op jit(solution)/shard_map/while
  205.5 6.0 %copy-start.4 = (bf16[1536,4,128]{0,2,1:T(8,128)(2,1)S(1)}, bf16[1536,4,128]{0,2,1:T(8,128)(2,1)}, u32[]{:S(2)}) copy-start(bf16[1536,4,128]{0,2,1:T(8,128)(2,1)} %get-tuple-element.294) | copy-start | bytes 4718596 | tf_op jit(solution)/shard_map/while
  216.5 1.0 copy-start.2
  219.4 6.0 %copy-start.1 = (bf16[1024,4,128]{0,2,1:T(8,128)(2,1)S(1)}, bf16[1024,4,128]{0,2,1:T(8,128)(2,1)}, u32[]{:S(2)}) copy-start(bf16[1024,4,128]{0,2,1:T(8,128)(2,1)} %get-tuple-element.281) | copy-start | bytes 3145732 | tf_op jit(solution)/shard_map/while
  219.4 6.0 %copy-start.4 = (bf16[1536,4,128]{0,2,1:T(8,128)(2,1)S(1)}, bf16[1536,4,128]{0,2,1:T(8,128)(2,1)}, u32[]{:S(2)}) copy-start(bf16[1536,4,128]{0,2,1:T(8,128)(2,1)} %get-tuple-element.294) | copy-start | bytes 4718596 | tf_op jit(solution)/shard_map/while
  230.4 1.0 copy-start.2
  234.4 94.1 %all-to-all-start.3 = ((bf16[8,128,512]{2,1,0:T(8,128)(2,1)}), bf16[8,128,512]{2,1,0:T(8,128)(2,1)S(1)}, u32[]{:S(2)}, u32[]{:S(2)}) async-start(bf16[8,128,512]{2,1,0:T(8,128)(2,1)} %copy.160), calls=%async_computation.3 | async-start | bytes 2097152 | tf_op jit(solution)/shard_map/all_to_all | solution.py:178
  243.2 7.6 %copy-start.3 = (f32[128,8,128]{0,2,1:T(8,128)S(1)}, f32[128,8,128]{0,2,1:T(8,128)}, u32[]{:S(2)}) copy-start(f32[128,8,128]{0,2,1:T(8,128)} %get-tuple-element.214) | copy-start | bytes 1572868
  251.8 32.8 %collective-permute-start.8 = (f32[128,1024]{1,0:T(8,128)}, f32[128,1024]{1,0:T(8,128)}, u32[]{:S(2)}, u32[]{:S(2)}) collective-permute-start(f32[128,1024]{1,0:T(8,128)} %copy.136), channel_id=1, source_target_pairs={{1,0},{2,1},{3,2},{4,3},{5,4},{6,5},{7,6},{9,8},{10,9},{11,10},{12... | collective-permute-start | bytes 1572872 | tf_op jit(solution)/shard_map/ppermute | solution.py:12
  262.1 24.9 %collective-permute-start.13 = (f32[128,1024]{1,0:T(8,128)}, f32[128,1024]{1,0:T(8,128)}, u32[]{:S(2)}, u32[]{:S(2)}) collective-permute-start(f32[128,1024]{1,0:T(8,128)} %copy.145), channel_id=1, source_target_pairs={{2,0},{3,1},{4,2},{5,3},{6,4},{7,5},{10,8},{11,9},{12,10},{13,11},... | collective-permute-start | bytes 1572872 | tf_op jit(solution)/shard_map/ppermute | solution.py:12
  263.4 29.0 %collective-permute-start.14 = (f32[128,1024]{1,0:T(8,128)}, f32[128,1024]{1,0:T(8,128)}, u32[]{:S(2)}, u32[]{:S(2)}) collective-permute-start(f32[128,1024]{1,0:T(8,128)} %copy.146), channel_id=1, source_target_pairs={{3,0},{4,1},{5,2},{6,3},{7,4},{11,8},{12,9},{13,10},{14,11},{15,12... | collective-permute-start | bytes 1572872 | tf_op jit(solution)/shard_map/ppermute | solution.py:12
  264.7 61.4 %collective-permute-start.15 = (f32[128,1024]{1,0:T(8,128)}, f32[128,1024]{1,0:T(8,128)}, u32[]{:S(2)}, u32[]{:S(2)}) collective-permute-start(f32[128,1024]{1,0:T(8,128)} %copy.147), channel_id=1, source_target_pairs={{4,0},{5,1},{6,2},{7,3},{12,8},{13,9},{14,10},{15,11},{20,16},{21,... | collective-permute-start | bytes 1572872 | tf_op jit(solution)/shard_map/ppermute | solution.py:12
  266.0 60.1 %collective-permute-start.12 = (f32[128,1024]{1,0:T(8,128)}, f32[128,1024]{1,0:T(8,128)}, u32[]{:S(2)}, u32[]{:S(2)}) collective-permute-start(f32[128,1024]{1,0:T(8,128)} %copy.143), channel_id=1, source_target_pairs={{1,0},{2,1},{3,2},{4,3},{5,4},{6,5},{7,6},{9,8},{10,9},{11,10},{12... | collective-permute-start | bytes 1572872 | tf_op jit(solution)/shard_map/ppermute | solution.py:12
where the time goes:
time: 336 us; the launch traced here: 330 us
  starting transfers between devices  75.4 us (22%)
  matrix products  66.5 us (20%)
  blocking collectives  58.8 us (18%)
  local copies, waits for them, and re-layouts  57.2 us (17%)
  waiting for transfers between devices  49.6 us (15%)
  other arithmetic  21.1 us (6%)
    psum x1, blocking collectives, body(): flag_total = lax.psum(jnp.sum(flags.astype(jnp.float32)), ('fsdp', 'seq'))  58.8 us
    ppermute x16, waiting for transfers between devices, passed_along(): return lax.ppermute(block, axis, route)  49.6 us
    ppermute x16, starting transfers between devices, passed_along(): return lax.ppermute(block, axis, route)  34.6 us
    all_to_all x1, starting transfers between devices, body(): lax.all_to_all(q_next, 'seq', split_axis=1, concat_axis=0, tiled=True)  21.4 us
    dot_general x1, matrix products, backward_local(): jnp.einsum('jgqk,qjgd->kjd', d_scores, grouped_q, preferred_element_type=...  16.4 us
    dot_general x1, matrix products, backward_local(): jnp.einsum('jgqk,kjd->qjgd', d_scores, k_window, preferred_element_type=j...  15.3 us
    unnamed x26, local copies, waits for them, and re-layouts  14.9 us
    sub x2, other arithmetic, masked_probs(): expo_vals = jnp.exp(scores - row_max)  12 us
  transfers between devices with their start and end apart: 20, of which 3 were waited for; matrix products, arithmetic and copies ran while one was open for 42% of the time, Pallas kernels for 0%

commit v1 on v0

v1 whole, which is shorter than its diff:
```python
import functools
import math

import jax
import jax.numpy as jnp
from jax import lax
from jax.experimental import pallas as pl
from jax.experimental.pallas import tpu as pltpu
from jax.sharding import PartitionSpec as P

HEAD_DIM = 128
SEG_MOST = 512
SLOTS = 5
NEG = -1e30


def shifted(block, step):
    size = lax.axis_size("seq")
    return lax.ppermute(
        block, "seq", [(i, i + step) for i in range(size) if 0 <= i + step < size]
    )


def swapped(block, from_even=True, from_odd=True):
    size = lax.axis_size("seq")
    route = [(i, i ^ 1) for i in range(size) if (from_odd if i % 2 else from_even)]
    return lax.ppermute(block, "seq", route)


def total_over(value, axis):
    size, step = lax.axis_size(axis), 1
    while step < size:
        route = [(i, i ^ step) for i in range(size)]
        value = value + lax.ppermute(value, axis, route)
        step *= 2
    return value


def mask_bias(seq_ids, rows_here):
    index = lax.axis_index("seq")
    odd = index % 2
    first = index * rows_here
    q_seg = lax.dynamic_slice_in_dim(seq_ids, first, rows_here)
    start = jnp.sum((seq_ids[:, None] < q_seg[None, :]).astype(jnp.int32), axis=0)
    q_pos = first + jnp.arange(rows_here, dtype=jnp.int32)
    back = jnp.stack(
        [
            jnp.int32(4),
            3 - 2 * odd,
            jnp.int32(2),
            1 + 2 * odd,
            jnp.int32(0),
        ]
    )
    k_pos = (first - back * rows_here)[:, None] + jnp.arange(rows_here, dtype=jnp.int32)
    k_pos = k_pos[:, :, None]
    keep = (k_pos >= start) & (k_pos <= q_pos)
    return jnp.where(keep, 0.0, NEG).astype(jnp.float32).reshape(SLOTS * rows_here, rows_here)


def gather_window(odd, refs, columns):
    far, far_x, mid, near_y, own, near_x = refs
    x_slot = jnp.where(odd == 1, near_x[:, columns], far_x[:, columns])
    return jnp.concatenate(
        [far[:, columns], x_slot, mid[:, columns], near_y[:, columns], own[:, columns]], axis=0
    )


def column(start):
    return pl.ds(pl.multiple_of(start, HEAD_DIM), HEAD_DIM)


def stacked_heads(ref, kv_head, group):
    return jnp.concatenate(
        [ref[:, column((kv_head * group + t) * HEAD_DIM)] for t in range(group)], axis=0
    )


def exp_scores(keys, queries, bias, group, factor):
    scores = lax.dot_general(
        keys, queries, (((1,), (1,)), ((), ())), preferred_element_type=jnp.float32
    )
    scores = scores * factor + jnp.concatenate([bias] * group, axis=1)
    return jnp.exp2(scores - jnp.max(scores, axis=0, keepdims=True))


def forward_kernel(group, kv_heads, factor, odd_ref, bias_ref, q_ref, *refs):
    window, out_ref = refs[:6], refs[6]
    odd = odd_ref[0]

    def one(g, carry):
        keys = gather_window(odd, window, column(g * HEAD_DIM))
        values = gather_window(odd, window, column((kv_heads + g) * HEAD_DIM))
        queries = stacked_heads(q_ref, g, group)
        expo = exp_scores(keys, queries, bias_ref[...], group, factor)
        total = jnp.sum(expo, axis=0, keepdims=True)
        out = lax.dot_general(
            values,
            expo.astype(jnp.bfloat16),
            (((0,), (0,)), ((), ())),
            preferred_element_type=jnp.float32,
        )
        out = out * (1.0 / total)
        rows = q_ref.shape[0]
        for t in range(group):
            out_ref[:, column((g * group + t) * HEAD_DIM)] = (
                out[:, t * rows : (t + 1) * rows].T.astype(out_ref.dtype)
            )
        return carry

    lax.fori_loop(0, kv_heads, one, 0)


def backward_kernel(group, kv_heads, factor, scale, odd_ref, bias_ref, q_ref, d_ref, *refs):
    window, dq_ref, outs = refs[:6], refs[6], refs[7:]
    odd = odd_ref[0]
    rows = q_ref.shape[0]

    def one(g, carry):
        k_col, v_col = column(g * HEAD_DIM), column((kv_heads + g) * HEAD_DIM)
        keys = gather_window(odd, window, k_col)
        values = gather_window(odd, window, v_col)
        queries = stacked_heads(q_ref, g, group)
        cots = stacked_heads(d_ref, g, group)
        expo = exp_scores(keys, queries, bias_ref[...], group, factor)
        d_probs = lax.dot_general(
            values, cots, (((1,), (1,)), ((), ())), preferred_element_type=jnp.float32
        )
        probs = expo * (1.0 / jnp.sum(expo, axis=0, keepdims=True))
        delta = jnp.sum(probs * d_probs, axis=0, keepdims=True)
        d_scores = (probs * (d_probs - delta) * scale).astype(jnp.bfloat16)
        dv = jnp.dot(probs.astype(jnp.bfloat16), cots, preferred_element_type=jnp.float32)
        dk = jnp.dot(d_scores, queries, preferred_element_type=jnp.float32)
        dq = lax.dot_general(
            keys, d_scores, (((0,), (0,)), ((), ())), preferred_element_type=jnp.float32
        )
        for t in range(group):
            dq_ref[:, column((g * group + t) * HEAD_DIM)] = (
                dq[:, t * rows : (t + 1) * rows].T.astype(dq_ref.dtype)
            )
        for s, ref in enumerate(outs):
            ref[:, k_col] = dk[s * rows : (s + 1) * rows].astype(ref.dtype)
            ref[:, v_col] = dv[s * rows : (s + 1) * rows].astype(ref.dtype)
        return carry

    lax.fori_loop(0, kv_heads, one, 0)


def call(kernel, outs, smem, *args):
    vmem = pl.BlockSpec(memory_space=pltpu.VMEM)
    return pl.pallas_call(
        kernel,
        out_shape=outs,
        in_specs=[pl.BlockSpec(memory_space=pltpu.SMEM)] + [vmem] * len(args),
        out_specs=jax.tree.map(lambda _: vmem, outs),
        compiler_params=pltpu.CompilerParams(vmem_limit_bytes=48 << 20),
    )(smem, *args)


def fetch_window(kv):
    mid = shifted(kv, 2)
    near_x = swapped(kv, from_odd=False)
    far = shifted(mid, 2)
    near_y = swapped(mid)
    far_x = swapped(far, from_even=False)
    return far, far_x, mid, near_y, kv, near_x


def body(q_next, k_next, v_next, seg_next, q_prev, k_prev, v_prev, seg_prev, upstream, flags):
    rows_here = q_next.shape[0]
    heads_all = q_next.shape[1] // HEAD_DIM
    kv_heads = k_next.shape[1] // HEAD_DIM
    group = heads_all // kv_heads
    seq_size = lax.axis_size("seq")
    token_total = rows_here * lax.axis_size("fsdp") * seq_size
    assert seq_size % 2 == 0 and SEG_MOST <= 4 * rows_here
    scale = HEAD_DIM ** (-0.5)
    factor = scale * math.log2(math.e)
    odd = lax.axis_index("seq") % 2
    odd_s = odd.reshape(1).astype(jnp.int32)

    kv_prev = jnp.concatenate([k_prev, v_prev], axis=1)
    kv_next = jnp.concatenate([k_next, v_next], axis=1)
    window_prev = fetch_window(kv_prev)
    window_next = fetch_window(kv_next)

    count = jnp.sum(flags.astype(jnp.float32)).reshape(1, 1) * jnp.ones((1, 128), jnp.float32)
    flag_total = total_over(total_over(count, "fsdp"), "seq")[0, 0]
    weight = flags.reshape(rows_here, 1).astype(jnp.float32) * (
        token_total / jnp.maximum(flag_total, 1.0)
    )
    cotangent = (upstream.astype(jnp.float32) * weight).astype(jnp.bfloat16)
    bias_prev = mask_bias(seg_prev[0], rows_here)
    bias_next = mask_bias(seg_next[0], rows_here)

    kv_shape = kv_prev.shape
    f32_kv = jax.ShapeDtypeStruct(kv_shape, jnp.float32)
    b16_kv = jax.ShapeDtypeStruct(kv_shape, jnp.bfloat16)
    q_shape = jax.ShapeDtypeStruct(q_prev.shape, jnp.bfloat16)
    grad_q, far, x_part, mid, y_part, own = call(
        functools.partial(backward_kernel, group, kv_heads, factor, scale),
        (q_shape, f32_kv, b16_kv, f32_kv, b16_kv, f32_kv),
        odd_s,
        bias_prev,
        q_prev,
        cotangent,
        *window_prev,
    )
    x_back = swapped(x_part).astype(jnp.float32)
    y_back = swapped(y_part).astype(jnp.float32)
    is_odd = odd == 1
    far = (far + jnp.where(is_odd, x_back, 0.0)).astype(jnp.bfloat16)
    mid = (mid + y_back + shifted(far, -2).astype(jnp.float32)).astype(jnp.bfloat16)
    own = own + jnp.where(is_odd, 0.0, x_back) + shifted(mid, -2).astype(jnp.float32)
    own = own.astype(jnp.bfloat16)
    split = k_prev.shape[1]

    attn_next = call(
        functools.partial(forward_kernel, group, kv_heads, factor),
        q_shape,
        odd_s,
        bias_next,
        q_next,
        *window_next,
    )
    return (attn_next, grad_q, own[:, :split], own[:, split:])


def solution(mesh):
    tokens = P(("fsdp", "seq"), None)
    ids = P("fsdp", None)
    return jax.shard_map(
        body,
        mesh=mesh,
        in_specs=(tokens, tokens, tokens, ids) * 2 + (tokens, P("fsdp", "seq")),
        out_specs=(tokens,) * 4,
        check_vma=False,
    )
```

time: 336 us -> 103 us (0.31); the launches traced: 330 us -> 103 us
  matrix products: 66.5 us -> 0 us
  blocking collectives: 58.8 us -> 0 us
  local copies, waits for them, and re-layouts: 57.2 us -> 6.25 us
  starting transfers between devices: 75.4 us -> 33.1 us
  Pallas kernels: 0 us -> 23.7 us
  waiting for transfers between devices: 49.6 us -> 32.9 us
  other arithmetic: 21.1 us -> 5.61 us
    psum x1 -> x0, blocking collectives: 58.8 us -> none  [body(): flag_total = lax.psum(jnp.sum(flags.astype(jnp.float32)), ('fsdp', 'seq'))]
    dot_general x8 -> x0, matrix products: 57.5 us -> none  [the longest x1 16.4 us: backward_local(): jnp.einsum('jgqk,qjgd->kjd', d_scores, grouped_q, preferred_element_type=...]
    all_to_all x4 -> x0, starting transfers between devices: 40.8 us -> none  [the longest x1 21.4 us: body(): lax.all_to_all(q_next, 'seq', split_axis=1, concat_axis=0, tiled=True)]
    pallas_call x0 -> x2, Pallas kernels: none -> 23.7 us  [call(): pl.pallas_call(kernel, out_shape=outs, in_specs=[pl.BlockSpec(memory_spac...]
    ppermute x16 -> x19, waiting for transfers between devices: 49.6 us -> 32.9 us  [the longest x6 17.5 us: shifted(): lax.ppermute(block, 'seq', [(i, i + step) for i in range(size) if 0 <= i...]
    slice x12 -> x1, local copies, waits for them, and re-layouts: 16.1 us -> 0.83 us  [body(): return (attn_next, grad_q, own[:, :split], own[:, split:])]
    sub x2 -> x1, other arithmetic: 12 us -> 0.01 us  [mask_bias(): first - back * rows_here]
    unnamed x26 -> x24, local copies, waits for them, and re-layouts: 14.9 us -> 3.7 us
  transfers between devices with their start and end apart: 20 -> 19, of which waited for: 3 -> 7; matrix products, arithmetic and copies ran while one was open for 42% -> 6% of each run, Pallas kernels for 0% -> 23%
where the time goes in v1:
time: 103 us
  starting transfers between devices  33.1 us (32%)
  waiting for transfers between devices  32.9 us (32%)
  Pallas kernels  23.7 us (23%)
  local copies, waits for them, and re-layouts  6.25 us (6%)
  other arithmetic  5.61 us (5%)
  between operations  1.08 us (1%)
    pallas_call x2, Pallas kernels, call(): pl.pallas_call(kernel, out_shape=outs, in_specs=[pl.BlockSpec(memory_spac...  23.7 us
    ppermute x6, starting transfers between devices, shifted(): lax.ppermute(block, 'seq', [(i, i + step) for i in range(size) if 0 <= i...  17.9 us
    ppermute x6, waiting for transfers between devices, shifted(): lax.ppermute(block, 'seq', [(i, i + step) for i in range(size) if 0 <= i...  17.5 us
    ppermute x5, waiting for transfers between devices, total_over(): value = value + lax.ppermute(value, axis, route)  15.4 us
    ppermute x8, starting transfers between devices, swapped(): return lax.ppermute(block, 'seq', route)  7.9 us
    ppermute x5, starting transfers between devices, total_over(): value = value + lax.ppermute(value, axis, route)  7.35 us
    unnamed x24, local copies, waits for them, and re-layouts  3.7 us
    convert_element_type x1, other arithmetic, body(): cotangent = (upstream.astype(jnp.float32) * weight).astype(jnp.bfloat16)  2.45 us
  transfers between devices with their start and end apart: 19, of which 7 were waited for; matrix products, arithmetic and copies ran while one was open for 6% of the time, Pallas kernels for 23%

profile of v1, /device:TPU:0, one launch (start us, length us, event | category | flops | bytes accessed | tf_op | source)
XLA Modules:
  0.0 102.7 jit_solution(969613109694367057)
XLA Ops:
  0.7 1.0 constant_dynamic-update-slice_fusion.3
  1.7 1.0 constant_dynamic-update-slice_fusion.2.refs_4_
  2.7 5.0 %collective-permute-start.10 = (bf16[128,2048]{1,0:T(8,128)(2,1)S(1)}, bf16[128,2048]{1,0:T(8,128)(2,1)S(1)}, u32[]{:S(2)}, u32[]{:S(2)}) collective-permute-start(bf16[128,2048]{1,0:T(8,128)(2,1)S(1)} %constant_dynamic-update-slice_fusion.2.refs_4_), channel_id=1, source_target_pairs={{0,2},{1,3},{2,4},{3,5},{4,6},{5,7},{8,10},{9,11},{10,12},{11,13},... | collective-permute-start | bytes 1572872 | tf_op jit(solution)/shard_map/ppermute | solution.py:19
  7.7 1.5 %collective-permute-start.14 = (bf16[128,2048]{1,0:T(8,128)(2,1)S(1)}, bf16[128,2048]{1,0:T(8,128)(2,1)S(1)}, u32[]{:S(2)}, u32[]{:S(2)}) collective-permute-start(bf16[128,2048]{1,0:T(8,128)(2,1)S(1)} %constant_dynamic-update-slice_fusion.2.refs_4_), channel_id=1, source_target_pairs={{0,1},{2,3},{4,5},{6,7},{8,9},{10,11},{12,13},{14,15},{16,17},{18,... | collective-permute-start | bytes 1572872 | tf_op jit(solution)/shard_map/ppermute | solution.py:27
  9.2 0.6 convert_reduce_fusion.2
  9.8 0.6 mul.48
  10.4 1.6 %collective-permute-start.5 = (f32[1,128]{1,0:T(1,128)S(1)}, f32[1,128]{1,0:T(1,128)S(1)}, u32[]{:S(2)}, u32[]{:S(2)}) collective-permute-start(f32[1,128]{1,0:T(1,128)S(1)} %mul.48), channel_id=1, source_target_pairs={{0,8},{8,0},{16,24},{24,16},{1,9},{9,1},{17,25},{25,17},{2,10},{10... | collective-permute-start | bytes 1544 | tf_op jit(solution)/shard_map/ppermute | solution.py:34
  12.1 3.5 %collective-permute-start = (bf16[128,2048]{1,0:T(8,128)(2,1)S(1)}, bf16[128,2048]{1,0:T(8,128)(2,1)S(1)}, u32[]{:S(2)}, u32[]{:S(2)}) collective-permute-start(bf16[128,2048]{1,0:T(8,128)(2,1)S(1)} %constant_dynamic-update-slice_fusion.refs_4_), channel_id=1, source_target_pairs={{0,2},{1,3},{2,4},{3,5},{4,6},{5,7},{8,10},{9,11},{10,12},{11,13},... | collective-permute-start | bytes 1572872 | tf_op jit(solution)/shard_map/ppermute | solution.py:19
  15.6 0.1 stack.14
  15.7 0.1 add_bitcast_fusion
  15.7 0.0 collective-permute-done.5
  15.7 0.7 broadcast_add_fusion
  16.4 1.6 %collective-permute-start.6 = (f32[1,128]{1,0:T(1,128)S(1)}, f32[1,128]{1,0:T(1,128)S(1)}, u32[]{:S(2)}, u32[]{:S(2)}) collective-permute-start(f32[1,128]{1,0:T(1,128)S(1)} %broadcast_add_fusion), channel_id=1, source_target_pairs={{0,16},{8,24},{16,0},{24,8},{1,17},{9,25},{17,1},{25,9},{2,18},{10... | collective-permute-start | bytes 1544 | tf_op jit(solution)/shard_map/ppermute | solution.py:34
  18.0 0.2 convert_reduce_fusion
  18.2 1.8 %collective-permute-done.6 = f32[1,128]{1,0:T(1,128)S(1)} collective-permute-done((f32[1,128]{1,0:T(1,128)S(1)}, f32[1,128]{1,0:T(1,128)S(1)}, u32[]{:S(2)}, u32[]{:S(2)}) %collective-permute-start.6) | collective-permute-done | bytes 544 | tf_op jit(solution)/shard_map/ppermute | solution.py:34
  20.0 0.6 fusion.8
  20.7 0.1 collective-permute-start.7
  20.8 0.2 convert_reduce_fusion.1
  21.0 0.9 collective-permute-done.7
  21.9 1.5 %collective-permute-start.8 = (f32[1,128]{1,0:T(1,128)S(1)}, f32[1,128]{1,0:T(1,128)S(1)}, u32[]{:S(2)}, u32[]{:S(2)}) collective-permute-start(f32[1,128]{1,0:T(1,128)S(1)} %add.94), channel_id=1, source_target_pairs={{0,2},{1,3},{2,0},{3,1},{4,6},{5,7},{6,4},{7,5},{8,10},{9,11},{10,... | collective-permute-start | bytes 1544 | tf_op jit(solution)/shard_map/ppermute | solution.py:34
  23.5 2.4 %collective-permute-start.11 = (bf16[128,2048]{1,0:T(8,128)(2,1)S(1)}, bf16[128,2048]{1,0:T(8,128)(2,1)S(1)}, u32[]{:S(2)}, u32[]{:S(2)}) collective-permute-start(bf16[128,2048]{1,0:T(8,128)(2,1)S(1)} %collective-permute-done.10.refs_2_), channel_id=1, source_target_pairs={{0,2},{1,3},{2,4},{3,5},{4,6},{5,7},{8,10},{9,11},{10,12},{11,13},... | collective-permute-start | bytes 1572872 | tf_op jit(solution)/shard_map/ppermute | solution.py:19
  25.9 5.3 %collective-permute-done.8 = f32[1,128]{1,0:T(1,128)S(1)} collective-permute-done((f32[1,128]{1,0:T(1,128)S(1)}, f32[1,128]{1,0:T(1,128)S(1)}, u32[]{:S(2)}, u32[]{:S(2)}) %collective-permute-start.8) | collective-permute-done | bytes 544 | tf_op jit(solution)/shard_map/ppermute | solution.py:34
  31.2 2.6 %collective-permute-start.9 = (f32[1,128]{1,0:T(1,128)S(1)}, f32[1,128]{1,0:T(1,128)S(1)}, u32[]{:S(2)}, u32[]{:S(2)}) collective-permute-start(f32[1,128]{1,0:T(1,128)S(1)} %add.95), channel_id=1, source_target_pairs={{0,4},{1,5},{2,6},{3,7},{4,0},{5,1},{6,2},{7,3},{8,12},{9,13},{10,... | collective-permute-start | bytes 1544 | tf_op jit(solution)/shard_map/ppermute | solution.py:34
  33.8 0.2 fusion.6
  34.0 7.3 %collective-permute-done.9 = f32[1,128]{1,0:T(1,128)S(1)} collective-permute-done((f32[1,128]{1,0:T(1,128)S(1)}, f32[1,128]{1,0:T(1,128)S(1)}, u32[]{:S(2)}, u32[]{:S(2)}) %collective-permute-start.9) | collective-permute-done | bytes 544 | tf_op jit(solution)/shard_map/ppermute | solution.py:34
  41.4 0.1 collective-permute-start.13
  41.5 1.3 %collective-permute-start.12 = (bf16[128,2048]{1,0:T(8,128)(2,1)S(1)}, bf16[128,2048]{1,0:T(8,128)(2,1)S(1)}, u32[]{:S(2)}, u32[]{:S(2)}) collective-permute-start(bf16[128,2048]{1,0:T(8,128)(2,1)S(1)} %collective-permute-done.11.refs_0_), channel_id=1, source_target_pairs={{1,0},{3,2},{5,4},{7,6},{9,8},{11,10},{13,12},{15,14},{17,16},{19,... | collective-permute-start | bytes 1572872 | tf_op jit(solution)/shard_map/ppermute | solution.py:27
  42.8 2.5 %multiply_convert_fusion.d_ref = bf16[128,4096]{1,0:T(8,128)(2,1)} fusion(bf16[128,4096]{1,0:T(8,128)(2,1)} %param.18, f32[128]{0:T(128)S(1)} %multiply_bitcast_fusion), kind=kLoop, calls=%fused_computation | loop fusion | flops 1572864 | bytes 2097664 | tf_op jit(solution)/shard_map/convert_element_type | solution.py:192
  45.3 0.8 copy-done.1
  46.1 1.0 %copy-done.2 = bf16[128,2048]{1,0:T(8,128)(2,1)S(1)} copy-done((bf16[128,2048]{1,0:T(8,128)(2,1)S(1)}, bf16[128,2048]{1,0:T(8,128)(2,1)}, u32[]{:S(2)}) %copy-start.2) | copy-done | bytes 524312
  47.1 16.1 %shard_map.130 = (bf16[128,4096]{1,0:T(8,128)(2,1)}, f32[128,2048]{1,0:T(8,128)S(1)}, bf16[128,2048]{1,0:T(8,128)(2,1)}, f32[128,2048]{1,0:T(8,128)}, bf16[128,2...) custom-call(s32[1]{0:T(128)} %bitcast.odd_ref, f32[640,128]{1,0:T(8,128)S(1)} %get-tuple-element.18.bias_ref, ...), custom_call_target="tpu_custom_call" | custom-call | tf_op jit(solution)/shard_map/pallas_call | solution.py:151
  63.2 0.8 copy-done.3
  64.0 1.2 %collective-permute-start.15 = (bf16[128,2048]{1,0:T(8,128)(2,1)}, bf16[128,2048]{1,0:T(8,128)(2,1)S(1)}, u32[]{:S(2)}, u32[]{:S(2)}) collective-permute-start(bf16[128,2048]{1,0:T(8,128)(2,1)} %get-tuple-element.12), channel_id=1, source_target_pairs={{0,1},{1,0},{2,3},{3,2},{4,5},{5,4},{6,7},{7,6},{8,9},{9,8},{10,11... | collective-permute-start | bytes 1572872 | tf_op jit(solution)/shard_map/ppermute | solution.py:27
  65.2 4.1 %collective-permute-start.1 = (bf16[128,2048]{1,0:T(8,128)(2,1)S(1)}, bf16[128,2048]{1,0:T(8,128)(2,1)S(1)}, u32[]{:S(2)}, u32[]{:S(2)}) collective-permute-start(bf16[128,2048]{1,0:T(8,128)(2,1)S(1)} %collective-permute-done.refs_2_), channel_id=1, source_target_pairs={{0,2},{1,3},{2,4},{3,5},{4,6},{5,7},{8,10},{9,11},{10,12},{11,13},... | collective-permute-start | bytes 1572872 | tf_op jit(solution)/shard_map/ppermute | solution.py:19
  69.4 0.1 collective-permute-start.16
  69.5 0.1 fusion.4
  69.6 1.4 %collective-permute-start.17 = (bf16[128,2048]{1,0:T(8,128)(2,1)S(1)}, bf16[128,2048]{1,0:T(8,128)(2,1)S(1)}, u32[]{:S(2)}, u32[]{:S(2)}) collective-permute-start(bf16[128,2048]{1,0:T(8,128)(2,1)S(1)} %fusion.4), channel_id=1, source_target_pairs={{2,0},{3,1},{4,2},{5,3},{6,4},{7,5},{10,8},{11,9},{12,10},{13,11},... | collective-permute-start | bytes 1572872 | tf_op jit(solution)/shard_map/ppermute | solution.py:19
  71.0 2.4 %collective-permute-start.4 = (bf16[128,2048]{1,0:T(8,128)(2,1)S(1)}, bf16[128,2048]{1,0:T(8,128)(2,1)S(1)}, u32[]{:S(2)}, u32[]{:S(2)}) collective-permute-start(bf16[128,2048]{1,0:T(8,128)(2,1)S(1)} %constant_dynamic-update-slice_fusion.refs_4_), channel_id=1, source_target_pairs={{0,1},{2,3},{4,5},{6,7},{8,9},{10,11},{12,13},{14,15},{16,17},{18,... | collective-permute-start | bytes 1572872 | tf_op jit(solution)/shard_map/ppermute | solution.py:27
  73.5 0.1 collective-permute-start.3
  73.5 7.1 %collective-permute-done.1.refs_0_ = bf16[128,2048]{1,0:T(8,128)(2,1)S(1)} collective-permute-done((bf16[128,2048]{1,0:T(8,128)(2,1)S(1)}, bf16[128,2048]{1,0:T(8,128)(2,1)S(1)}, u32[]{:S(2)}, u32[]{:S(2)}) %collective-permute-start.1) | collective-permute-done | bytes 524320 | tf_op jit(solution)/shard_map/ppermute | solution.py:19
  80.7 1.3 %collective-permute-start.2 = (bf16[128,2048]{1,0:T(8,128)(2,1)S(1)}, bf16[128,2048]{1,0:T(8,128)(2,1)S(1)}, u32[]{:S(2)}, u32[]{:S(2)}) collective-permute-start(bf16[128,2048]{1,0:T(8,128)(2,1)S(1)} %collective-permute-done.1.refs_0_), channel_id=1, source_target_pairs={{1,0},{3,2},{5,4},{7,6},{9,8},{11,10},{13,12},{15,14},{17,16},{19,... | collective-permute-start | bytes 1572872 | tf_op jit(solution)/shard_map/ppermute | solution.py:27
  82.0 4.0 %collective-permute-done.17 = bf16[128,2048]{1,0:T(8,128)(2,1)S(1)} collective-permute-done((bf16[128,2048]{1,0:T(8,128)(2,1)S(1)}, bf16[128,2048]{1,0:T(8,128)(2,1)S(1)}, u32[]{:S(2)}, u32[]{:S(2)}) %collective-permute-start.17) | collective-permute-done | bytes 524320 | tf_op jit(solution)/shard_map/ppermute | solution.py:19
  85.9 0.2 add_convert_fusion
  86.1 1.4 %collective-permute-start.18 = (bf16[128,2048]{1,0:T(8,128)(2,1)S(1)}, bf16[128,2048]{1,0:T(8,128)(2,1)S(1)}, u32[]{:S(2)}, u32[]{:S(2)}) collective-permute-start(bf16[128,2048]{1,0:T(8,128)(2,1)S(1)} %add_convert_fusion), channel_id=1, source_target_pairs={{2,0},{3,1},{4,2},{5,3},{6,4},{7,5},{10,8},{11,9},{12,10},{13,11},... | collective-permute-start | bytes 1572872 | tf_op jit(solution)/shard_map/ppermute | solution.py:19
  87.6 7.6 %shard_map.129 = bf16[128,4096]{1,0:T(8,128)(2,1)} custom-call(s32[1]{0:T(128)} %bitcast.odd_ref, f32[640,128]{1,0:T(8,128)S(1)} %get-tuple-element.19.bias_ref, bf16[128,4096]{1,0:T(8,128)(2,1)S(1)} %copy-done, bf16[128,2048]{1,0:T(8,128)(2,1)S(1)} %collective-permute-done.1.refs_0_, bf16[128,2048]{1,0:T(8,128)(2,1)S(1)} %collective-permute-done.2.refs_1_, ...), custom_call_target="tpu_custom_call" | custom-call | tf_op jit(solution)/shard_map/pallas_call | solution.py:151
  95.3 6.4 %collective-permute-done.18 = bf16[128,2048]{1,0:T(8,128)(2,1)S(1)} collective-permute-done((bf16[128,2048]{1,0:T(8,128)(2,1)S(1)}, bf16[128,2048]{1,0:T(8,128)(2,1)S(1)}, u32[]{:S(2)}, u32[]{:S(2)}) %collective-permute-start.18) | collective-permute-done | bytes 524320 | tf_op jit(solution)/shard_map/ppermute | solution.py:19
  101.6 0.2 fusion.2
  101.8 0.8 fusion.7
  (39 shorter events, 0.1 us)
Async XLA Ops:
  0.6 8.5 %copy-start.10 = (s32[1,128]{1,0:T(1,128)S(1)}, s32[1,128]{1,0:T(1,128)}, u32[]{:S(2)}) copy-start(s32[1,128]{1,0:T(1,128)} %param.19) | copy-start | bytes 1540
  0.6 11.4 %copy-start.6 = (bf16[128,1024]{1,0:T(8,128)(2,1)S(1)}, bf16[128,1024]{1,0:T(8,128)(2,1)}, u32[]{:S(2)}) copy-start(bf16[128,1024]{1,0:T(8,128)(2,1)} %param.11) | copy-start | bytes 786436
  0.7 11.4 %copy-start.7 = (bf16[128,1024]{1,0:T(8,128)(2,1)S(1)}, bf16[128,1024]{1,0:T(8,128)(2,1)}, u32[]{:S(2)}) copy-start(bf16[128,1024]{1,0:T(8,128)(2,1)} %param.12) | copy-start | bytes 786436
  0.7 15.1 %copy-start.9 = (s32[1,1024]{1,0:T(1,128)S(1)}, s32[1,1024]{1,0:T(1,128)}, u32[]{:S(2)}) copy-start(s32[1,1024]{1,0:T(1,128)} %param.13) | copy-start | bytes 12292
  0.7 15.1 %copy-start.8 = (s32[1,1024]{1,0:T(1,128)S(1)}, s32[1,1024]{1,0:T(1,128)}, u32[]{:S(2)}) copy-start(s32[1,1024]{1,0:T(1,128)} %param.17) | copy-start | bytes 12292
  2.7 20.8 %collective-permute-start.10 = (bf16[128,2048]{1,0:T(8,128)(2,1)S(1)}, bf16[128,2048]{1,0:T(8,128)(2,1)S(1)}, u32[]{:S(2)}, u32[]{:S(2)}) collective-permute-start(bf16[128,2048]{1,0:T(8,128)(2,1)S(1)} %constant_dynamic-update-slice_fusion.2.refs_4_), channel_id=1, source_target_pairs={{0,2},{1,3},{2,4},{3,5},{4,6},{5,7},{8,10},{9,11},{10,12},{11,13},... | collective-permute-start | bytes 1572872 | tf_op jit(solution)/shard_map/ppermute | solution.py:19
  7.7 37.6 %collective-permute-start.14 = (bf16[128,2048]{1,0:T(8,128)(2,1)S(1)}, bf16[128,2048]{1,0:T(8,128)(2,1)S(1)}, u32[]{:S(2)}, u32[]{:S(2)}) collective-permute-start(bf16[128,2048]{1,0:T(8,128)(2,1)S(1)} %constant_dynamic-update-slice_fusion.2.refs_4_), channel_id=1, source_target_pairs={{0,1},{2,3},{4,5},{6,7},{8,9},{10,11},{12,13},{14,15},{16,17},{18,... | collective-permute-start | bytes 1572872 | tf_op jit(solution)/shard_map/ppermute | solution.py:27
  10.4 5.3 %collective-permute-start.5 = (f32[1,128]{1,0:T(1,128)S(1)}, f32[1,128]{1,0:T(1,128)S(1)}, u32[]{:S(2)}, u32[]{:S(2)}) collective-permute-start(f32[1,128]{1,0:T(1,128)S(1)} %mul.48), channel_id=1, source_target_pairs={{0,8},{8,0},{16,24},{24,16},{1,9},{9,1},{17,25},{25,17},{2,10},{10... | collective-permute-start | bytes 1544 | tf_op jit(solution)/shard_map/ppermute | solution.py:34
  12.1 53.2 %collective-permute-start = (bf16[128,2048]{1,0:T(8,128)(2,1)S(1)}, bf16[128,2048]{1,0:T(8,128)(2,1)S(1)}, u32[]{:S(2)}, u32[]{:S(2)}) collective-permute-start(bf16[128,2048]{1,0:T(8,128)(2,1)S(1)} %constant_dynamic-update-slice_fusion.refs_4_), channel_id=1, source_target_pairs={{0,2},{1,3},{2,4},{3,5},{4,6},{5,7},{8,10},{9,11},{10,12},{11,13},... | collective-permute-start | bytes 1572872 | tf_op jit(solution)/shard_map/ppermute | solution.py:19
  16.4 3.6 %collective-permute-start.6 = (f32[1,128]{1,0:T(1,128)S(1)}, f32[1,128]{1,0:T(1,128)S(1)}, u32[]{:S(2)}, u32[]{:S(2)}) collective-permute-start(f32[1,128]{1,0:T(1,128)S(1)} %broadcast_add_fusion), channel_id=1, source_target_pairs={{0,16},{8,24},{16,0},{24,8},{1,17},{9,25},{17,1},{25,9},{2,18},{10... | collective-permute-start | bytes 1544 | tf_op jit(solution)/shard_map/ppermute | solution.py:34
  20.7 1.2 %collective-permute-start.7 = (f32[1,128]{1,0:T(1,128)S(1)}, f32[1,128]{1,0:T(1,128)S(1)}, u32[]{:S(2)}, u32[]{:S(2)}) collective-permute-start(f32[1,128]{1,0:T(1,128)S(1)} %fusion.8), channel_id=1, source_target_pairs={{0,1},{1,0},{2,3},{3,2},{4,5},{5,4},{6,7},{7,6},{8,9},{9,8},{10,11... | collective-permute-start | bytes 1544 | tf_op jit(solution)/shard_map/ppermute | solution.py:34
  21.9 9.3 %collective-permute-start.8 = (f32[1,128]{1,0:T(1,128)S(1)}, f32[1,128]{1,0:T(1,128)S(1)}, u32[]{:S(2)}, u32[]{:S(2)}) collective-permute-start(f32[1,128]{1,0:T(1,128)S(1)} %add.94), channel_id=1, source_target_pairs={{0,2},{1,3},{2,0},{3,1},{4,6},{5,7},{6,4},{7,5},{8,10},{9,11},{10,... | collective-permute-start | bytes 1544 | tf_op jit(solution)/shard_map/ppermute | solution.py:34
  23.5 18.0 %collective-permute-start.11 = (bf16[128,2048]{1,0:T(8,128)(2,1)S(1)}, bf16[128,2048]{1,0:T(8,128)(2,1)S(1)}, u32[]{:S(2)}, u32[]{:S(2)}) collective-permute-start(bf16[128,2048]{1,0:T(8,128)(2,1)S(1)} %collective-permute-done.10.refs_2_), channel_id=1, source_target_pairs={{0,2},{1,3},{2,4},{3,5},{4,6},{5,7},{8,10},{9,11},{10,12},{11,13},... | collective-permute-start | bytes 1572872 | tf_op jit(solution)/shard_map/ppermute | solution.py:19
  31.2 10.1 %collective-permute-start.9 = (f32[1,128]{1,0:T(1,128)S(1)}, f32[1,128]{1,0:T(1,128)S(1)}, u32[]{:S(2)}, u32[]{:S(2)}) collective-permute-start(f32[1,128]{1,0:T(1,128)S(1)} %add.95), channel_id=1, source_target_pairs={{0,4},{1,5},{2,6},{3,7},{4,0},{5,1},{6,2},{7,3},{8,12},{9,13},{10,... | collective-permute-start | bytes 1544 | tf_op jit(solution)/shard_map/ppermute | solution.py:34
  41.4 4.6 %collective-permute-start.13 = (bf16[128,2048]{1,0:T(8,128)(2,1)S(1)}, bf16[128,2048]{1,0:T(8,128)(2,1)S(1)}, u32[]{:S(2)}, u32[]{:S(2)}) collective-permute-start(bf16[128,2048]{1,0:T(8,128)(2,1)S(1)} %collective-permute-done.10.refs_2_), channel_id=1, source_target_pairs={{0,1},{1,0},{2,3},{3,2},{4,5},{5,4},{6,7},{7,6},{8,9},{9,8},{10,11... | collective-permute-start | bytes 1572872 | tf_op jit(solution)/shard_map/ppermute | solution.py:27
  41.5 4.6 %collective-permute-start.12 = (bf16[128,2048]{1,0:T(8,128)(2,1)S(1)}, bf16[128,2048]{1,0:T(8,128)(2,1)S(1)}, u32[]{:S(2)}, u32[]{:S(2)}) collective-permute-start(bf16[128,2048]{1,0:T(8,128)(2,1)S(1)} %collective-permute-done.11.refs_0_), channel_id=1, source_target_pairs={{1,0},{3,2},{5,4},{7,6},{9,8},{11,10},{13,12},{15,14},{17,16},{19,... | collective-permute-start | bytes 1572872 | tf_op jit(solution)/shard_map/ppermute | solution.py:27
  45.3 0.8 copy-start.1
  46.1 1.0 %copy-start.2 = (bf16[128,2048]{1,0:T(8,128)(2,1)S(1)}, bf16[128,2048]{1,0:T(8,128)(2,1)}, u32[]{:S(2)}) copy-start(bf16[128,2048]{1,0:T(8,128)(2,1)} %copy-done.1) | copy-start | bytes 1572868
  63.2 0.8 copy-start.3
  64.0 5.4 %collective-permute-start.15 = (bf16[128,2048]{1,0:T(8,128)(2,1)}, bf16[128,2048]{1,0:T(8,128)(2,1)S(1)}, u32[]{:S(2)}, u32[]{:S(2)}) collective-permute-start(bf16[128,2048]{1,0:T(8,128)(2,1)} %get-tuple-element.12), channel_id=1, source_target_pairs={{0,1},{1,0},{2,3},{3,2},{4,5},{5,4},{6,7},{7,6},{8,9},{9,8},{10,11... | collective-permute-start | bytes 1572872 | tf_op jit(solution)/shard_map/ppermute | solution.py:27
  65.2 15.4 %collective-permute-start.1 = (bf16[128,2048]{1,0:T(8,128)(2,1)S(1)}, bf16[128,2048]{1,0:T(8,128)(2,1)S(1)}, u32[]{:S(2)}, u32[]{:S(2)}) collective-permute-start(bf16[128,2048]{1,0:T(8,128)(2,1)S(1)} %collective-permute-done.refs_2_), channel_id=1, source_target_pairs={{0,2},{1,3},{2,4},{3,5},{4,6},{5,7},{8,10},{9,11},{10,12},{11,13},... | collective-permute-start | bytes 1572872 | tf_op jit(solution)/shard_map/ppermute | solution.py:19
  69.4 12.6 %collective-permute-start.16 = (bf16[128,2048]{1,0:T(8,128)(2,1)}, bf16[128,2048]{1,0:T(8,128)(2,1)S(1)}, u32[]{:S(2)}, u32[]{:S(2)}) collective-permute-start(bf16[128,2048]{1,0:T(8,128)(2,1)} %copy-done.3), channel_id=1, source_target_pairs={{0,1},{1,0},{2,3},{3,2},{4,5},{5,4},{6,7},{7,6},{8,9},{9,8},{10,11... | collective-permute-start | bytes 1572872 | tf_op jit(solution)/shard_map/ppermute | solution.py:27
  69.4 16.5 %copy-start.5 = (f32[128,2048]{1,0:T(8,128)S(1)}, f32[128,2048]{1,0:T(8,128)}, u32[]{:S(2)}) copy-start(f32[128,2048]{1,0:T(8,128)} %get-tuple-element.13) | copy-start | bytes 3145732
  69.6 16.3 %collective-permute-start.17 = (bf16[128,2048]{1,0:T(8,128)(2,1)S(1)}, bf16[128,2048]{1,0:T(8,128)(2,1)S(1)}, u32[]{:S(2)}, u32[]{:S(2)}) collective-permute-start(bf16[128,2048]{1,0:T(8,128)(2,1)S(1)} %fusion.4), channel_id=1, source_target_pairs={{2,0},{3,1},{4,2},{5,3},{6,4},{7,5},{10,8},{11,9},{12,10},{13,11},... | collective-permute-start | bytes 1572872 | tf_op jit(solution)/shard_map/ppermute | solution.py:19
  71.0 16.5 %collective-permute-start.4 = (bf16[128,2048]{1,0:T(8,128)(2,1)S(1)}, bf16[128,2048]{1,0:T(8,128)(2,1)S(1)}, u32[]{:S(2)}, u32[]{:S(2)}) collective-permute-start(bf16[128,2048]{1,0:T(8,128)(2,1)S(1)} %constant_dynamic-update-slice_fusion.refs_4_), channel_id=1, source_target_pairs={{0,1},{2,3},{4,5},{6,7},{8,9},{10,11},{12,13},{14,15},{16,17},{18,... | collective-permute-start | bytes 1572872 | tf_op jit(solution)/shard_map/ppermute | solution.py:27
  73.5 14.1 %collective-permute-start.3 = (bf16[128,2048]{1,0:T(8,128)(2,1)S(1)}, bf16[128,2048]{1,0:T(8,128)(2,1)S(1)}, u32[]{:S(2)}, u32[]{:S(2)}) collective-permute-start(bf16[128,2048]{1,0:T(8,128)(2,1)S(1)} %collective-permute-done.refs_2_), channel_id=1, source_target_pairs={{0,1},{1,0},{2,3},{3,2},{4,5},{5,4},{6,7},{7,6},{8,9},{9,8},{10,11... | collective-permute-start | bytes 1572872 | tf_op jit(solution)/shard_map/ppermute | solution.py:27
  80.7 6.9 %collective-permute-start.2 = (bf16[128,2048]{1,0:T(8,128)(2,1)S(1)}, bf16[128,2048]{1,0:T(8,128)(2,1)S(1)}, u32[]{:S(2)}, u32[]{:S(2)}) collective-permute-start(bf16[128,2048]{1,0:T(8,128)(2,1)S(1)} %collective-permute-done.1.refs_0_), channel_id=1, source_target_pairs={{1,0},{3,2},{5,4},{7,6},{9,8},{11,10},{13,12},{15,14},{17,16},{19,... | collective-permute-start | bytes 1572872 | tf_op jit(solution)/shard_map/ppermute | solution.py:27
  85.9 1.7 %copy-start = (bf16[128,4096]{1,0:T(8,128)(2,1)S(1)}, bf16[128,4096]{1,0:T(8,128)(2,1)}, u32[]{:S(2)}) copy-start(bf16[128,4096]{1,0:T(8,128)(2,1)} %q_ref.2) | copy-start | bytes 3145732
  86.1 15.5 %collective-permute-start.18 = (bf16[128,2048]{1,0:T(8,128)(2,1)S(1)}, bf16[128,2048]{1,0:T(8,128)(2,1)S(1)}, u32[]{:S(2)}, u32[]{:S(2)}) collective-permute-start(bf16[128,2048]{1,0:T(8,128)(2,1)S(1)} %add_convert_fusion), channel_id=1, source_target_pairs={{2,0},{3,1},{4,2},{5,3},{6,4},{7,5},{10,8},{11,9},{12,10},{13,11},... | collective-permute-start | bytes 1572872 | tf_op jit(solution)/shard_map/ppermute | solution.py:19
  87.6 14.0 %copy-start.4 = (f32[128,2048]{1,0:T(8,128)S(1)}, f32[128,2048]{1,0:T(8,128)}, u32[]{:S(2)}) copy-start(f32[128,2048]{1,0:T(8,128)} %get-tuple-element.11) | copy-start | bytes 3145732
